TPU v7x, 16 devices: a whole 2x2x2 slice. The times are simulated.
16 devices in a mesh: dep: 2 (over z), col: 2 (over y), row: 4 (over x, core).
Axes of the slice: x: 2, y: 2, z: 2, core: 2. Of those that a mesh axis runs over, the one named last changes fastest.
Arguments:
- a_mat: bfloat16 [5120, 5120], P('row', 'col')
- b_mat: bfloat16 [5120, 5120], P('row', 'col')
Outputs:
- output: float32 [5120, 5120], P('row', ('col', 'dep'))
All inputs are finite; a program needn't handle non-finite values.
Results may differ from a plain program's by a relative error of at most 0.001.
Values are sent between devices in bfloat16 or wider.
A program may use at most 1 GiB of HBM per device.

v0:
```python
import jax
import jax.numpy as jnp
from jax import lax
from jax.sharding import PartitionSpec as P


def solution(mesh):
    n_dep = mesh.shape['dep']
    n_row = mesh.shape['row']
    n_col = mesh.shape['col']

    def local_product(a_blk, b_blk):
        layer_idx = lax.axis_index('dep')
        rows_a, cols_a = a_blk.shape
        cols_b = b_blk.shape[1]
        unit_len = cols_a // (n_row * n_dep)
        a_part = a_blk.reshape(rows_a, n_row, n_dep, unit_len)
        a_part = lax.dynamic_index_in_dim(a_part, layer_idx, axis=2, keepdims=False)
        a_part = a_part.reshape(rows_a, n_row * unit_len)
        b_part = b_blk.reshape(n_col, n_dep, unit_len, cols_b)
        b_part = lax.dynamic_index_in_dim(b_part, layer_idx, axis=1, keepdims=False)
        b_part = b_part.reshape(n_col * unit_len, cols_b)
        a_panel = lax.all_gather(a_part, 'col', axis=1, tiled=True)
        b_panel = lax.all_gather(b_part, 'row', axis=0, tiled=True)
        part_sum = jnp.dot(a_panel, b_panel, preferred_element_type=jnp.float32)
        return lax.psum_scatter(part_sum, 'dep', scatter_dimension=1, tiled=True)

    return jax.shard_map(local_product, mesh=mesh, in_specs=(P('row', 'col'), P('row', 'col')), out_specs=P('row', ('col', 'dep')), check_vma=False)
```

profile of v0, /device:TPU:0, one launch (start us, length us, event | category | flops | bytes accessed | tf_op | source)
XLA Modules:
  0.0 368.6 jit_solution(4248432631586336321)
XLA Ops:
  6.5 0.0 all-gather.3.cloned.1.call-start
  6.5 9.5 %copy.3 = bf16[1280,2560]{0,1:T(8,128)(2,1)} copy(bf16[1280,2560]{1,0:T(8,128)(2,1)} %param.2) | data formatting | bytes 13107200 | tf_op args[0]
  16.0 3.8 %constant_dynamic-slice_fusion.1 = bf16[1280,4,1,320]{0,3,2,1:T(8,128)(2,1)} fusion(bf16[1280,4,2,320]{0,3,2,1:T(8,128)(2,1)} %bitcast.6, s32[]{:T(128)S(6)} %select_n.6), kind=kLoop, calls=%fused_computation.1 | loop fusion | bytes 6553604 | tf_op jit(solution)/shard_map/jit(dynamic_index_in_dim)/dynamic_slice | solution.py:18
  19.8 0.0 all-gather.3.cloned.1.call-update
  19.9 0.0 all-gather.5.cloned.1.call-start
  19.9 3.9 %constant_dynamic-slice_fusion = bf16[2,1,320,2560]{3,2,1,0:T(8,128)(2,1)} fusion(bf16[2,2,320,2560]{3,2,1,0:T(8,128)(2,1)} %bitcast.9, s32[]{:T(128)S(6)} %select_n.6), kind=kLoop, calls=%fused_computation | loop fusion | bytes 6553604 | tf_op jit(solution)/shard_map/jit(dynamic_index_in_dim)/dynamic_slice | solution.py:21
  23.8 0.0 all-gather.5.cloned.1.call-update
  23.8 0.0 reduce-scatter.2.cloned.1.call-start
  23.8 81.1 %all-gather.3.cloned.1.call-done = bf16[1280,2560]{0,1:T(8,128)(2,1)} async-done(((bf16[1280,1280]{0,1:T(8,128)(2,1)}), bf16[1280,2560]{0,1:T(8,128)(2,1)}) %all-gather.3.cloned.1.call-update) | async-done | bytes 6553616 | tf_op jit(solution)/shard_map/all_gather | solution.py:23
  105.0 85.5 %all-gather.5.cloned.1.call-done = bf16[2560,2560]{1,0:T(8,128)(2,1)} async-done(((bf16[640,2560]{1,0:T(8,128)(2,1)}), bf16[2560,2560]{1,0:T(8,128)(2,1)}) %all-gather.5.cloned.1.call-update) | async-done | bytes 13107216 | tf_op jit(solution)/shard_map/all_gather | solution.py:24
  190.4 23.3 %fusion = f32[1280,2560]{1,0:T(8,128)} fusion(bf16[1280,2560]{0,1:T(8,128)(2,1)} %all-gather.3.cloned.1.call-done, bf16[2560,2560]{1,0:T(8,128)(2,1)} %all-gather.5.cloned.1.call-done), kind=kOutput, calls=%fused_computation.2 | convolution fusion | flops 16777216000 | bytes 32768000 | tf_op jit(solution)/shard_map/dot_general | solution.py:25
  213.7 0.0 reduce-scatter.2.cloned.1.call-update
  213.7 148.4 %reduce-scatter.2.cloned.1.call-done = f32[1280,1280]{1,0:T(8,128)} async-done(((f32[1280,2560]{1,0:T(8,128)}), f32[1280,1280]{1,0:T(8,128)}) %reduce-scatter.2.cloned.1.call-update) | async-done | bytes 6553616 | tf_op jit(solution)/shard_map/reduce_scatter | solution.py:26
Async XLA Ops:
  6.5 98.4 %all-gather.3.cloned.1.call-start = ((), (), s32[]{:S(2)}) async-start(), calls=%async_computation.1 | async-start | bytes 9830400 | tf_op jit(solution)/shard_map/all_gather | solution.py:23
  19.9 170.6 %all-gather.5.cloned.1.call-start = ((), (), s32[]{:S(2)}) async-start(), calls=%async_computation.2 | async-start | bytes 16384000 | tf_op jit(solution)/shard_map/all_gather | solution.py:24
  23.8 338.3 %reduce-scatter.2.cloned.1.call-start = ((), (), s32[]{:S(2)}) async-start(), calls=%async_computation.3 | async-start | bytes 19660800 | tf_op jit(solution)/shard_map/reduce_scatter | solution.py:26
Sparse Core Ops, SparseCore 0:
  20.0 84.9 all-gather.2
  106.5 83.8 all-gather.4
  213.8 148.2 reduce-scatter.1
where the time goes:
time: 369 us
  waiting for transfers between devices  315 us (85%)
  matrix products  23.3 us (6%)
  local copies, waits for them, and re-layouts  17.1 us (5%)
  between operations  13.1 us (4%)
    reduce_scatter x1, waiting for transfers between devices, local_product(): return lax.psum_scatter(part_sum, 'dep', scatter_dimension=1, tiled=True)  148 us
    all_gather x1, waiting for transfers between devices, local_product(): b_panel = lax.all_gather(b_part, 'row', axis=0, tiled=True)  85.5 us
    all_gather x1, waiting for transfers between devices, local_product(): a_panel = lax.all_gather(a_part, 'col', axis=1, tiled=True)  81.1 us
    dot_general x1, matrix products, local_product(): part_sum = jnp.dot(a_panel, b_panel, preferred_element_type=jnp.float32)  23.3 us
    unnamed x1, local copies, waits for them, and re-layouts  9.48 us
  transfers between devices with their start and end apart: 3, of which 3 were waited for; matrix products, arithmetic and copies ran while one was open for 1% of the time, Pallas kernels for 0%

commit v1 on v0

v1 whole, which is shorter than its diff:
```python
import functools

import jax
import jax.numpy as jnp
from jax import lax
from jax.experimental import pallas as pl
from jax.experimental.pallas import tpu as pltpu
from jax.sharding import PartitionSpec as P

MESH = pl.DeviceIdType.MESH
STEPS = 10
SUBS = 5
CHUNK = 128
ROWS = 256
COLS = 256
TOTAL = STEPS * SUBS
AHEAD = 6
LAG_IN = 4
LAG = 8


def _kernel(a_ref, b_ref, c_ref, abuf, bbuf, ys, yr, zs, zr, xs, xr, ds, dr, bs, br, la, lb):
    z, y, r = lax.axis_index("dep"), lax.axis_index("col"), lax.axis_index("row")
    quarter = a_ref.shape[1] // 2
    across = lax.rem(r + 2, 4)
    peer = r + 1 - 2 * lax.rem(r, 2)
    peer_across = lax.rem(peer + 2, 4)
    to_y, to_z, to_x, to_d = {"col": 1 - y}, {"dep": 1 - z}, {"row": across}, {"row": peer}

    def lanes(q):
        return pl.ds(pl.multiple_of(q * CHUNK, CHUNK), CHUNK)

    def remote(src, dst, send, recv, to):
        return pltpu.make_async_remote_copy(
            src_ref=src, dst_ref=dst, send_sem=send, recv_sem=recv, device_id=to, device_id_type=MESH
        )

    def a_slot(t, s, q):
        return abuf.at[t, pl.ds(s * ROWS, ROWS), lanes(q)]

    def b_slot(t, s, q):
        return bbuf.at[t, lanes(q), pl.ds(s * COLS, COLS)]

    def y_copy(t, s, part=z, sem=None):
        sem = t * SUBS + s if sem is None else sem
        src = a_ref.at[pl.ds(s * ROWS, ROWS), pl.ds(pl.multiple_of(part * quarter + t * CHUNK, CHUNK), CHUNK)]
        return remote(src, a_slot(t, s, 2 * y + part), ys.at[sem], yr.at[sem], to_y)

    def y_in(t, s, part=z, sem=None):
        sem = t * SUBS + s if sem is None else sem
        slot = a_slot(t, s, 2 * (1 - y) + part)
        return remote(slot, slot, ys.at[sem], yr.at[sem], to_y)

    def z_copy(t, s):
        slot = a_slot(t, s, 2 * (1 - y) + z)
        return remote(slot, slot, zs.at[t * SUBS + s], zr.at[t * SUBS + s], to_z)

    def z_in(t, s):
        slot = a_slot(t, s, 2 * (1 - y) + 1 - z)
        return remote(slot, slot, zs.at[t * SUBS + s], zr.at[t * SUBS + s], to_z)

    def x_copy(t, s):
        src = b_ref.at[
            pl.ds(pl.multiple_of(t * CHUNK, CHUNK), CHUNK),
            pl.ds(pl.multiple_of(z * quarter + s * COLS, CHUNK), COLS),
        ]
        return remote(src, b_slot(t, s, r), xs.at[t * SUBS + s], xr.at[t * SUBS + s], to_x)

    def x_in(t, s):
        slot = b_slot(t, s, across)
        return remote(slot, slot, xs.at[t * SUBS + s], xr.at[t * SUBS + s], to_x)

    def d_copy(t, s):
        slot = b_slot(t, s, across)
        return remote(slot, slot, ds.at[t * SUBS + s], dr.at[t * SUBS + s], to_d)

    def d_in(t, s):
        slot = b_slot(t, s, peer_across)
        return remote(slot, slot, ds.at[t * SUBS + s], dr.at[t * SUBS + s], to_d)

    def b_rows(t):
        return b_ref.at[
            pl.ds(pl.multiple_of(t * CHUNK, CHUNK), CHUNK), pl.ds(pl.multiple_of(z * quarter, CHUNK), quarter)
        ]

    def peer_copy(t):
        return remote(b_rows(t), bbuf.at[t, lanes(r)], bs.at[t], br.at[t], to_d)

    def peer_in(t):
        slot = bbuf.at[t, lanes(peer)]
        return remote(slot, slot, bs.at[t], br.at[t], to_d)

    def b_load(t):
        return pltpu.make_async_copy(b_rows(t), bbuf.at[t, lanes(r)], lb.at[t])

    def a_load(t, part):
        src = a_ref.at[:, pl.ds(pl.multiple_of(part * quarter + t * CHUNK, CHUNK), CHUNK)]
        return pltpu.make_async_copy(src, abuf.at[t, :, lanes(2 * y + part)], la.at[2 * t + part])

    def step_of(n):
        return (n // SUBS, n % SUBS)

    def start_local(t):
        peer_copy(t).start()
        b_load(t).start()
        a_load(t, 0).start()
        a_load(t, 1).start()

    def wait_local(t):
        peer_copy(t).wait_send()
        peer_in(t).wait_recv()
        b_load(t).wait()
        a_load(t, 0).wait()
        a_load(t, 1).wait()

    def product(t, p):
        cols = pl.ds(p * COLS, COLS)
        c_ref[:, cols] += jnp.dot(abuf[t], bbuf[t, :, cols], preferred_element_type=jnp.float32)

    barrier = pltpu.get_barrier_semaphore()
    for to in (to_x, to_y, to_z, to_d):
        pl.semaphore_signal(barrier, inc=1, device_id=to, device_id_type=MESH)
    pl.semaphore_wait(barrier, 4)

    for n in range(AHEAD):
        y_copy(*step_of(n)).start()
        x_copy(*step_of(n)).start()
    start_local(0)
    start_local(1)
    c_ref[...] = jnp.zeros_like(c_ref)

    def arrive(t, s, last):
        y_in(t, s).wait_recv()
        if not (last and s == SUBS - 1):
            z_copy(t, s).start()
        x_in(t, s).wait_recv()
        d_copy(t, s).start()

    def settle(t, s):
        y_copy(t, s).wait_send()
        x_copy(t, s).wait_send()
        z_copy(t, s).wait_send()
        d_copy(t, s).wait_send()
        z_in(t, s).wait_recv()
        d_in(t, s).wait_recv()

    def body(t, carry):
        @pl.when(t + 2 < STEPS)
        def _():
            start_local(t + 2)

        for s in range(SUBS):
            arrive(t, s, False)

            dt, s2 = step_of(s + AHEAD)

            @pl.when(t + dt < STEPS)
            def _(dt=dt, s2=s2):
                y_copy(t + dt, s2).start()
                x_copy(t + dt, s2).start()

            dt, s2 = (s - LAG_IN) // SUBS, (s - LAG_IN) % SUBS

            @pl.when(t + dt >= 0)
            def _(dt=dt, s2=s2):
                settle(t + dt, s2)

            dt, s2 = (s - LAG) // SUBS, (s - LAG) % SUBS

            @pl.when(t + dt >= 0)
            def _(dt=dt, s2=s2):
                if s2 == 0:
                    wait_local(t + dt)
                product(t + dt, s2)

        return carry

    lax.fori_loop(0, STEPS - 1, body, 0)

    last = STEPS - 1
    done_in = last * SUBS - LAG_IN
    done_mul = last * SUBS - LAG
    extra = (last, SUBS - 1)
    y_copy(*extra, part=1 - z, sem=TOTAL).start()
    for s in range(SUBS):
        n = last * SUBS + s
        arrive(last, s, True)
        while done_in <= n - LAG_IN:
            settle(*step_of(done_in))
            done_in += 1
        while done_mul < done_in - SUBS + 1 and done_mul < last * SUBS:
            t, p = step_of(done_mul)
            if p == 0:
                wait_local(t)
            product(t, p)
            done_mul += 1
    while done_in < TOTAL:
        t, s = step_of(done_in)
        if done_in < TOTAL - 1:
            settle(t, s)
        else:
            y_copy(t, s).wait_send()
            x_copy(t, s).wait_send()
            d_copy(t, s).wait_send()
            d_in(t, s).wait_recv()
            y_copy(t, s, part=1 - z, sem=TOTAL).wait_send()
            y_in(t, s, part=1 - z, sem=TOTAL).wait_recv()
        done_in += 1
        while done_mul < done_in - SUBS + 1:
            t, p = step_of(done_mul)
            if p == 0:
                wait_local(t)
            product(t, p)
            done_mul += 1
    while done_mul < TOTAL:
        t, p = step_of(done_mul)
        if p == 0:
            wait_local(t)
        product(t, p)
        done_mul += 1


def solution(mesh):
    def local_product(a_blk, b_blk):
        rows, half = a_blk.shape
        piece = half // 2
        return pl.pallas_call(
            _kernel,
            out_shape=jax.ShapeDtypeStruct((rows, piece), jnp.float32),
            in_specs=[pl.BlockSpec(memory_space=pltpu.HBM)] * 2,
            out_specs=pl.BlockSpec(memory_space=pltpu.VMEM),
            scratch_shapes=[
                pltpu.VMEM((STEPS, rows, 4 * CHUNK), jnp.bfloat16),
                pltpu.VMEM((STEPS, 4 * CHUNK, piece), jnp.bfloat16),
                pltpu.SemaphoreType.DMA((TOTAL + 1,)),
                pltpu.SemaphoreType.DMA((TOTAL + 1,)),
                pltpu.SemaphoreType.DMA((TOTAL,)),
                pltpu.SemaphoreType.DMA((TOTAL,)),
                pltpu.SemaphoreType.DMA((TOTAL,)),
                pltpu.SemaphoreType.DMA((TOTAL,)),
                pltpu.SemaphoreType.DMA((TOTAL,)),
                pltpu.SemaphoreType.DMA((TOTAL,)),
                pltpu.SemaphoreType.DMA((STEPS,)),
                pltpu.SemaphoreType.DMA((STEPS,)),
                pltpu.SemaphoreType.DMA((2 * STEPS,)),
                pltpu.SemaphoreType.DMA((STEPS,)),
            ],
            compiler_params=pltpu.CompilerParams(collective_id=0, has_side_effects=True, vmem_limit_bytes=45 * 2**20),
            cost_estimate=pl.CostEstimate(flops=2 * rows * piece * 2 * half, bytes_accessed=40 * 2**20, transcendentals=0),
        )(a_blk, b_blk)

    return jax.shard_map(
        local_product,
        mesh=mesh,
        in_specs=(P("row", "col"), P("row", "col")),
        out_specs=P("row", ("col", "dep")),
        check_vma=False,
    )
```

time: 369 us -> 88.9 us (0.24)
  waiting for transfers between devices: 315 us -> 0 us
  Pallas kernels: 0 us -> 86 us
  matrix products: 23.3 us -> 0 us
  local copies, waits for them, and re-layouts: 17.1 us -> 2.79 us
  between operations: 13.1 us -> 0.01 us
    all_gather x2 -> x0, waiting for transfers between devices: 167 us -> none  [the longest x1 85.5 us: local_product(): b_panel = lax.all_gather(b_part, 'row', axis=0, tiled=True)]
    reduce_scatter x1 -> x0, waiting for transfers between devices: 148 us -> none  [local_product(): return lax.psum_scatter(part_sum, 'dep', scatter_dimension=1, tiled=True)]
    pallas_call x0 -> x1, Pallas kernels: none -> 86 us  [local_product(): pl.pallas_call(_kernel, out_shape=jax.ShapeDtypeStruct((rows, piece), jnp...]
    dot_general x1 -> x0, matrix products: 23.3 us -> none  [local_product(): part_sum = jnp.dot(a_panel, b_panel, preferred_element_type=jnp.float32)]
    dynamic_slice x2 -> x0, local copies, waits for them, and re-layouts: 7.67 us -> none  [the longest x1 3.86 us: local_product(): b_part = lax.dynamic_index_in_dim(b_part, layer_idx, axis=1, keepdims=False)]
    unnamed x1, local copies, waits for them, and re-layouts: 9.48 us -> 2.79 us
  transfers between devices with their start and end apart: 3 -> 0, of which waited for: 3 -> 0; matrix products, arithmetic and copies ran while one was open for 1% -> 0% of each run, Pallas kernels for 0% -> 0%
where the time goes in v1:
time: 88.9 us; the launch traced here: 88.8 us
  Pallas kernels  86 us (97%)
  local copies, waits for them, and re-layouts  2.79 us (3%)
    pallas_call x1, Pallas kernels, local_product(): pl.pallas_call(_kernel, out_shape=jax.ShapeDtypeStruct((rows, piece), jnp...  86 us
    unnamed x1, local copies, waits for them, and re-layouts  2.79 us

profile of v1, /device:TPU:0, one launch (start us, length us, event | category | flops | bytes accessed | tf_op | source)
XLA Modules:
  0.0 88.8 jit_solution(10721989034814000822)
XLA Ops:
  0.0 86.0 %shard_map.28 = f32[1280,1280]{1,0:T(8,128)S(1)} custom-call(bf16[1280,2560]{1,0:T(8,128)(2,1)} %a_ref.1, bf16[1280,2560]{1,0:T(8,128)(2,1)} %b_ref.1), custom_call_target="tpu_custom_call" | custom-call | flops 16777216000 | bytes 41943040 | tf_op jit(solution)/shard_map/pallas_call | solution.py:227
  86.0 2.8 %copy.4 = f32[1280,1280]{1,0:T(8,128)} copy(f32[1280,1280]{1,0:T(8,128)S(1)} %shard_map.28) | data formatting | bytes 13107200

commit v2 on v0

v2 whole, which is shorter than its diff:
```python
import jax
import jax.numpy as jnp
from jax import lax
from jax.experimental import pallas as pl
from jax.experimental.pallas import tpu as pltpu
from jax.sharding import PartitionSpec as P

MESH = pl.DeviceIdType.MESH
STEPS = 10
SUBS = 10
CHUNK = 128
PIECE = 128
COLS = 256
TOTAL = STEPS * SUBS
LAST = STEPS - 1
EXTRA = 3
AHEAD = 6
LAG = 6
RING = 2 * AHEAD
STEP_RING = 4
TAIL = (STEPS - 2) * SUBS
LIMIT = 42 * 2**20
LIMIT_FINISH = 20 * 2**20


def _exchange(a_ref, b_ref, c_ref, a_last, b_last, abuf, bbuf, yr, zr, xr, dr, sent, local):
    z, y, r = lax.axis_index("dep"), lax.axis_index("col"), lax.axis_index("row")
    quarter = a_ref.shape[1] // 2
    across = lax.rem(r + 2, 4)
    peer = r + 1 - 2 * lax.rem(r, 2)
    peer_across = lax.rem(peer + 2, 4)
    to_y, to_z, to_x, to_d = {"col": 1 - y}, {"dep": 1 - z}, {"row": across}, {"row": peer}

    def aligned(start, size):
        return pl.ds(pl.multiple_of(start, CHUNK), size)

    def lanes(q):
        return aligned(q * CHUNK, CHUNK)

    def remote(src, dst, send, recv, to):
        return pltpu.make_async_remote_copy(
            src_ref=src, dst_ref=dst, send_sem=send, recv_sem=recv, device_id=to, device_id_type=MESH
        )

    def is_last(t):
        return isinstance(t, int) and t == LAST

    def a_step(t):
        return a_last if is_last(t) else abuf.at[t]

    def b_step(t):
        return b_last if is_last(t) else bbuf.at[t]

    def a_slot(n, q):
        return a_step(n // SUBS).at[aligned((n % SUBS) * PIECE, PIECE), lanes(q)]

    def b_slot(n, q):
        return b_step(n // SUBS).at[lanes(q), aligned((n % SUBS) * PIECE, PIECE)]

    def take(some, sem):
        pltpu.make_async_copy(some, some, sem).wait()

    def step_sem(sems, t):
        return sems.at[STEP_RING if is_last(t) else lax.rem(t, STEP_RING)]

    def y_start(n):
        extra = isinstance(n, int) and n >= TOTAL
        part, send, recv = (1 - z, 4, RING) if extra else (z, 0, lax.rem(n, RING))
        n = n - EXTRA if extra else n
        src = a_ref.at[aligned((n % SUBS) * PIECE, PIECE), aligned(part * quarter + n // SUBS * CHUNK, CHUNK)]
        remote(src, a_slot(n, 2 * y + part), sent.at[send], yr.at[recv], to_y).start()

    def y_wait(n):
        take(a_slot(n, 2 * (1 - y) + z), yr.at[lax.rem(n, RING)])

    def z_start(n):
        slot = a_slot(n, 2 * (1 - y) + z)
        t = n // SUBS
        remote(slot, slot, sent.at[5 if is_last(t) else 1], step_sem(zr, t), to_z).start()

    def x_start(n):
        src = b_ref.at[aligned(n // SUBS * CHUNK, CHUNK), aligned(z * quarter + (n % SUBS) * PIECE, PIECE)]
        remote(src, b_slot(n, r), sent.at[2], xr.at[lax.rem(n, RING)], to_x).start()

    def x_wait(n):
        take(b_slot(n, across), xr.at[lax.rem(n, RING)])

    def d_start(n):
        slot = b_slot(n, across)
        remote(slot, slot, sent.at[3], step_sem(dr, n // SUBS), to_d).start()

    def settle(t):
        if is_last(t):
            take(a_last.at[pl.ds(0, (SUBS - EXTRA) * PIECE), lanes(2 * (1 - y) + 1 - z)], step_sem(zr, t))
            take(a_last.at[pl.ds(0, EXTRA * PIECE), lanes(2 * (1 - y) + 1 - z)], yr.at[RING])
        else:
            take(abuf.at[t, :, lanes(2 * (1 - y) + 1 - z)], step_sem(zr, t))
        take(b_step(t).at[lanes(peer_across)], step_sem(dr, t))

    def start_local():
        for t in range(STEPS):
            sems = 4 * (t // LAST)
            for part in range(2):
                src = a_ref.at[:, pl.ds(part * quarter + t * CHUNK, CHUNK)]
                pltpu.make_async_copy(src, a_step(t).at[:, lanes(2 * y + part)], local.at[sems]).start()
            src = b_ref.at[pl.ds(t * CHUNK, CHUNK), aligned(z * quarter, quarter)]
            dst = b_step(t).at[lanes(r)]
            pltpu.make_async_copy(src, dst, local.at[sems + 1]).start()
            remote(src, dst, local.at[sems + 2], local.at[sems + 3], to_d).start()

    def wait_local():
        take(abuf.at[:, :, pl.ds(0, 2 * CHUNK)], local.at[0])
        take(a_last.at[:, pl.ds(0, 2 * CHUNK)], local.at[4])
        for i, place in ((1, r), (2, r), (3, peer)):
            take(bbuf.at[:, lanes(place)], local.at[i])
            take(b_last.at[lanes(place)], local.at[4 + i])

    def product(t, p):
        cols = pl.ds(p * COLS, COLS)
        c_ref[:, cols] += jnp.dot(abuf[t], bbuf[t, :, cols], preferred_element_type=jnp.float32)

    barrier = pltpu.get_barrier_semaphore()
    for to in (to_x, to_y, to_z, to_d):
        pl.semaphore_signal(barrier, inc=1, device_id=to, device_id_type=MESH)
    pl.semaphore_wait(barrier, 4)

    for n in range(AHEAD):
        y_start(n)
        x_start(n)
    start_local()
    c_ref[...] = jnp.zeros_like(c_ref)

    def forward(n):
        known = isinstance(n, int)
        y_wait(n)
        if not known or n < TOTAL - EXTRA:
            z_start(n)
        if not known or n + AHEAD < TOTAL + EXTRA:
            y_start(n + AHEAD)
        x_wait(n)
        d_start(n)
        if not known or n + AHEAD < TOTAL:
            x_start(n + AHEAD)

    def body(t, carry):
        for s in range(SUBS):
            forward(t * SUBS + s)
            dt, i = (s - LAG) // SUBS - 1, (s - LAG) % SUBS
            if i % 2 == 0:

                @pl.when(t + dt >= 0)
                def _(dt=dt, i=i):
                    if i == 0:
                        pl.when(t + dt == 0)(wait_local)
                        settle(t + dt)
                    product(t + dt, i // 2)

        return carry

    lax.fori_loop(0, TAIL // SUBS, body, 0)

    work = [(t, p) for t in (STEPS - 4, STEPS - 3, STEPS - 2) for p in range(SUBS // 2)]
    begun = TAIL - (STEPS - 3) * SUBS - LAG
    work = work[(begun + 1) // 2 :]
    for n in range(TAIL, TOTAL):
        forward(n)
        t, p = work[0] if work else (LAST, 0)
        first = (t + 1) * SUBS + LAG
        if t < LAST and n >= first + (2 * p if t < LAST - 1 else p):
            if p == 0:
                settle(t)
            product(t, p)
            work.pop(0)
    for t, p in work:
        if p == 0:
            settle(t)
        product(t, p)
    settle(LAST)
    for i in (0, 2, 3):
        take(b_ref.at[:, pl.ds(0, quarter)], sent.at[i])
    take(abuf.at[:, :, pl.ds(0, CHUNK)], sent.at[1])
    take(a_last.at[pl.ds(0, EXTRA * PIECE), pl.ds(0, CHUNK)], sent.at[4])
    take(a_last.at[pl.ds(0, (SUBS - EXTRA) * PIECE), pl.ds(0, CHUNK)], sent.at[5])


def _finish(c_part, a_last, b_last, c_ref, done, sems):
    copies = []
    for i in range(SUBS):
        rows = pl.ds(i * PIECE, PIECE)
        done[rows] = c_part[rows] + jnp.dot(a_last[rows], b_last[...], preferred_element_type=jnp.float32)
        copies.append(pltpu.make_async_copy(done.at[rows], c_ref.at[rows], sems.at[i]))
        copies[-1].start()
    for copy in copies:
        copy.wait()


def solution(mesh):
    def local_product(a_blk, b_blk):
        rows, half = a_blk.shape
        piece = half // 2
        vmem = pl.BlockSpec(memory_space=pltpu.VMEM)
        hbm = pl.BlockSpec(memory_space=pltpu.HBM)
        parts = pl.pallas_call(
            _exchange,
            out_shape=[
                jax.ShapeDtypeStruct((rows, piece), jnp.float32),
                jax.ShapeDtypeStruct((rows, 4 * CHUNK), jnp.bfloat16),
                jax.ShapeDtypeStruct((4 * CHUNK, piece), jnp.bfloat16),
            ],
            in_specs=[hbm, hbm],
            out_specs=[vmem] * 3,
            scratch_shapes=[
                pltpu.VMEM((LAST, rows, 4 * CHUNK), jnp.bfloat16),
                pltpu.VMEM((LAST, 4 * CHUNK, piece), jnp.bfloat16),
                pltpu.SemaphoreType.DMA((RING + 1,)),
                pltpu.SemaphoreType.DMA((STEP_RING + 1,)),
                pltpu.SemaphoreType.DMA((RING,)),
                pltpu.SemaphoreType.DMA((STEP_RING + 1,)),
                pltpu.SemaphoreType.DMA((6,)),
                pltpu.SemaphoreType.DMA((8,)),
            ],
            compiler_params=pltpu.CompilerParams(collective_id=0, has_side_effects=True, vmem_limit_bytes=LIMIT),
        )(a_blk, b_blk)
        return pl.pallas_call(
            _finish,
            out_shape=jax.ShapeDtypeStruct((rows, piece), jnp.float32),
            in_specs=[vmem] * 3,
            out_specs=hbm,
            scratch_shapes=[pltpu.VMEM((rows, piece), jnp.float32), pltpu.SemaphoreType.DMA((SUBS,))],
            compiler_params=pltpu.CompilerParams(vmem_limit_bytes=LIMIT_FINISH),
        )(*parts)

    return jax.shard_map(
        local_product,
        mesh=mesh,
        in_specs=(P("row", "col"), P("row", "col")),
        out_specs=P("row", ("col", "dep")),
        check_vma=False,
    )
```

time: 369 us -> 81.6 us (0.22)
  waiting for transfers between devices: 315 us -> 0 us
  Pallas kernels: 0 us -> 81.5 us
  matrix products: 23.3 us -> 0 us
  local copies, waits for them, and re-layouts: 17.1 us -> 0 us
  between operations: 13.1 us -> 0.01 us
    all_gather x2 -> x0, waiting for transfers between devices: 167 us -> none  [the longest x1 85.5 us: local_product(): b_panel = lax.all_gather(b_part, 'row', axis=0, tiled=True)]
    reduce_scatter x1 -> x0, waiting for transfers between devices: 148 us -> none  [local_product(): return lax.psum_scatter(part_sum, 'dep', scatter_dimension=1, tiled=True)]
    pallas_call x0 -> x2, Pallas kernels: none -> 81.5 us  [the longest x1 78.3 us: local_product(): pl.pallas_call(_exchange, out_shape=[jax.ShapeDtypeStruct((rows, piece),...]
    dot_general x1 -> x0, matrix products: 23.3 us -> none  [local_product(): part_sum = jnp.dot(a_panel, b_panel, preferred_element_type=jnp.float32)]
    unnamed x1 -> x0, local copies, waits for them, and re-layouts: 9.48 us -> none
    dynamic_slice x2 -> x0, local copies, waits for them, and re-layouts: 7.67 us -> none  [the longest x1 3.86 us: local_product(): b_part = lax.dynamic_index_in_dim(b_part, layer_idx, axis=1, keepdims=False)]
  transfers between devices with their start and end apart: 3 -> 0, of which waited for: 3 -> 0; matrix products, arithmetic and copies ran while one was open for 1% -> 0% of each run, Pallas kernels for 0% -> 0%
where the time goes in v2:
time: 81.6 us; the launch traced here: 81.5 us
  Pallas kernels  81.5 us (100%)
    pallas_call x1, Pallas kernels, local_product(): pl.pallas_call(_exchange, out_shape=[jax.ShapeDtypeStruct((rows, piece),...  78.3 us
    pallas_call x1, Pallas kernels, local_product(): pl.pallas_call(_finish, out_shape=jax.ShapeDtypeStruct((rows, piece), jnp...  3.2 us

profile of v2, /device:TPU:0, one launch (start us, length us, event | category | flops | bytes accessed | tf_op | source)
XLA Modules:
  0.0 81.5 jit_solution(8826506278997423113)
XLA Ops:
  0.0 78.3 %shard_map.28 = (f32[1280,1280]{1,0:T(8,128)S(1)}, bf16[1280,512]{1,0:T(8,128)(2,1)S(1)}, bf16[512,1280]{1,0:T(8,128)(2,1)S(1)}) custom-call(bf16[1280,2560]{1,0:T(8,128)(2,1)} %a_ref.1, bf16[1280,2560]{1,0:T(8,128)(2,1)} %b_ref.1), custom_call_target="tpu_custom_call" | custom-call | tf_op jit(solution)/shard_map/pallas_call | solution.py:203
  78.3 3.2 %shard_map.29 = f32[1280,1280]{1,0:T(8,128)} custom-call(f32[1280,1280]{1,0:T(8,128)S(1)} %get-tuple-element.8.c_part, bf16[1280,512]{1,0:T(8,128)(2,1)S(1)} %get-tuple-element.9.a_last, bf16[512,1280]{1,0:T(8,128)(2,1)S(1)} %get-tuple-element.10.b_last), custom_call_target="tpu_custom_call" | custom-call | tf_op jit(solution)/shard_map/pallas_call | solution.py:224

commit v3 on v2

v3 whole, which is shorter than its diff:
```python
import jax
import jax.numpy as jnp
from jax import lax
from jax.experimental import pallas as pl
from jax.experimental.pallas import tpu as pltpu
from jax.sharding import PartitionSpec as P

MESH = pl.DeviceIdType.MESH
STEPS = 10
SUBS = 10
CHUNK = 128
PIECE = 128
COLS = 256
TOTAL = STEPS * SUBS
LAST = STEPS - 1
EXTRA = 384
EARLY = 3
AHEAD = 7
WIDE = 5
B_AHEAD = 2
LAG = 6
RING = 2 * AHEAD
B_RING = 2 * B_AHEAD
B_SUBS = SUBS // WIDE
B_TOTAL = STEPS * B_SUBS
STEP_RING = 3
TAIL = (STEPS - 2) * SUBS
LIMIT = 42 * 2**20
LIMIT_FINISH = 20 * 2**20


def _exchange(a_ref, b_ref, c_ref, a_last, b_last, abuf, bbuf, yr, zr, xr, dr, sent, local, ready):
    z, y, r = lax.axis_index("dep"), lax.axis_index("col"), lax.axis_index("row")
    quarter = a_ref.shape[1] // 2
    across = lax.rem(r + 2, 4)
    peer = r + 1 - 2 * lax.rem(r, 2)
    peer_across = lax.rem(peer + 2, 4)
    to_y, to_z, to_x, to_d = {"col": 1 - y}, {"dep": 1 - z}, {"row": across}, {"row": peer}

    def aligned(start, size):
        return pl.ds(pl.multiple_of(start, CHUNK), size)

    def lanes(q):
        return aligned(q * CHUNK, CHUNK)

    def remote(src, dst, send, recv, to):
        return pltpu.make_async_remote_copy(
            src_ref=src, dst_ref=dst, send_sem=send, recv_sem=recv, device_id=to, device_id_type=MESH
        )

    def is_last(t):
        return isinstance(t, int) and t == LAST

    def a_step(t):
        return a_last if is_last(t) else abuf.at[t]

    def b_step(t):
        return b_last if is_last(t) else bbuf.at[t]

    def a_slot(n, q):
        return a_step(n // SUBS).at[aligned((n % SUBS) * PIECE, PIECE), lanes(q)]

    def b_slot(n, q):
        return b_step(n // B_SUBS).at[lanes(q), aligned((n % B_SUBS) * WIDE * PIECE, WIDE * PIECE)]

    def take(some, sem):
        pltpu.make_async_copy(some, some, sem).wait()

    def step_sem(sems, t):
        return sems.at[lax.rem(t, STEP_RING)]

    def y_start(n):
        if isinstance(n, int) and n == TOTAL:
            rows = pl.ds(SUBS * PIECE - EXTRA, EXTRA)
            src = a_ref.at[rows, aligned((1 - z) * quarter + LAST * CHUNK, CHUNK)]
            remote(src, a_last.at[rows, lanes(2 * y + 1 - z)], sent.at[0], yr.at[RING], to_y).start()
            return
        src = a_ref.at[aligned((n % SUBS) * PIECE, PIECE), aligned(z * quarter + n // SUBS * CHUNK, CHUNK)]
        remote(src, a_slot(n, 2 * y + z), sent.at[0], yr.at[lax.rem(n, RING)], to_y).start()

    def y_wait(n):
        take(a_slot(n, 2 * (1 - y) + z), yr.at[lax.rem(n, RING)])

    def z_start(n):
        slot, recv = a_slot(n, 2 * (1 - y) + z), step_sem(zr, n // SUBS)
        if is_last(n // SUBS):
            i = n % SUBS
            size = min(PIECE, SUBS * PIECE - EXTRA - i * PIECE)
            if size <= 0:
                return
            slot = a_last.at[pl.ds(i * PIECE, size), lanes(2 * (1 - y) + z)]
            recv = zr.at[STEP_RING] if i < EARLY else recv
        remote(slot, slot, sent.at[0], recv, to_z).start()

    def x_start(n):
        columns = aligned(z * quarter + (n % B_SUBS) * WIDE * PIECE, WIDE * PIECE)
        src = b_ref.at[aligned(n // B_SUBS * CHUNK, CHUNK), columns]
        remote(src, b_slot(n, r), sent.at[1], xr.at[lax.rem(n, B_RING)], to_x).start()

    def x_wait(n):
        take(b_slot(n, across), xr.at[lax.rem(n, B_RING)])

    def d_start(n):
        slot = b_slot(n, across)
        remote(slot, slot, sent.at[1], step_sem(dr, n // B_SUBS), to_d).start()

    def settle(t):
        take(abuf.at[t, :, lanes(2 * (1 - y) + 1 - z)], step_sem(zr, t))
        take(bbuf.at[t, lanes(peer_across)], step_sem(dr, t))

    def start_local():
        for t in range(STEPS):
            for part in range(2):
                src = a_ref.at[:, pl.ds(part * quarter + t * CHUNK, CHUNK)]
                pltpu.make_async_copy(src, a_step(t).at[:, lanes(2 * y + part)], local.at[0]).start()
            src = b_ref.at[pl.ds(t * CHUNK, CHUNK), aligned(z * quarter, quarter)]
            dst = b_step(t).at[lanes(r)]
            pltpu.make_async_copy(src, dst, local.at[1]).start()
            remote(src, dst, local.at[2], local.at[3], to_d).start()

    def wait_local():
        take(a_ref, local.at[0])
        for i in (1, 2, 3):
            take(b_ref.at[:, pl.ds(0, quarter)], local.at[i])

    def product(t, p):
        cols = pl.ds(p * COLS, COLS)
        c_ref[:, cols] += jnp.dot(abuf[t], bbuf[t, :, cols], preferred_element_type=jnp.float32)

    x = r // 2
    axes = ((x, to_x), (y, to_y), (z, to_z))
    barrier = pltpu.get_barrier_semaphore()
    for at, to in axes:

        @pl.when(at == 0)
        def _(to=to):
            pl.semaphore_signal(barrier, inc=1, device_id=to, device_id_type=MESH)

    pl.semaphore_signal(barrier, inc=1, device_id=to_d, device_id_type=MESH)
    pl.semaphore_wait(barrier, 1 + x + y + z)
    for i, (at, to) in enumerate(axes):

        @pl.when(at == 1)
        def _(i=i, to=to):
            pl.semaphore_signal(ready.at[i], inc=1, device_id=to, device_id_type=MESH)

    def begin(i):
        for n in range((B_AHEAD, AHEAD)[i]):
            (x_start, y_start)[i](n)

    pl.when(y == 1)(lambda: begin(1))
    pl.when(x == 1)(lambda: begin(0))
    start_local()
    for i in (1, 0):

        @pl.when(axes[i][0] == 0)
        def _(i=i):
            pl.semaphore_wait(ready.at[i], 1)
            begin(i)

    pl.when(z == 0)(lambda: pl.semaphore_wait(ready.at[2], 1))
    c_ref[...] = jnp.zeros_like(c_ref)

    def forward(t, s):
        known = isinstance(t, int)
        n = t * SUBS + s
        y_wait(n)
        z_start(n)
        if not known or n + AHEAD <= TOTAL:
            y_start(n + AHEAD)
        if s % WIDE == WIDE - 1:
            m = t * B_SUBS + s // WIDE
            x_wait(m)
            d_start(m)
            if not known or m + B_AHEAD < B_TOTAL:
                x_start(m + B_AHEAD)

    def body(t, carry):
        for s in range(SUBS):
            forward(t, s)
            dt, i = (s - LAG) // SUBS - 1, (s - LAG) % SUBS
            if i % 2 == 0:

                @pl.when(t + dt >= 0)
                def _(dt=dt, i=i):
                    if i == 0:
                        pl.when(t + dt == 0)(wait_local)
                        settle(t + dt)
                    product(t + dt, i // 2)

        return carry

    lax.fori_loop(0, TAIL // SUBS, body, 0)

    work = [(t, p) for t in (STEPS - 4, STEPS - 3, STEPS - 2) for p in range(SUBS // 2)]
    begun = TAIL - (STEPS - 3) * SUBS - LAG
    work = work[(begun + 1) // 2 :]
    for n in range(TAIL, TOTAL):
        forward(n // SUBS, n % SUBS)
        t, p = work[0] if work else (LAST, 0)
        first = (t + 1) * SUBS + LAG
        if t < LAST and n >= first + (2 * p if t < LAST - 1 else p):
            if p == 0:
                settle(t)
            product(t, p)
            work.pop(0)
    for t, p in work:
        if p == 0:
            settle(t)
        product(t, p)
    mine = lanes(2 * (1 - y) + 1 - z)
    early = EARLY * PIECE
    take(b_last.at[lanes(peer_across)], step_sem(dr, LAST))
    take(a_last.at[pl.ds(0, early), mine], zr.at[STEP_RING])
    for i in range(EARLY):
        rows = pl.ds(i * PIECE, PIECE)
        c_ref[rows] += jnp.dot(a_last[rows], b_last[...], preferred_element_type=jnp.float32)
    take(a_last.at[pl.ds(early, SUBS * PIECE - EXTRA - early), mine], step_sem(zr, LAST))
    take(a_last.at[pl.ds(SUBS * PIECE - EXTRA, EXTRA), mine], yr.at[RING])
    take(a_ref, sent.at[0])
    take(b_ref, sent.at[1])


def _finish(c_part, a_last, b_last, c_ref, done, sem):
    early = pl.ds(0, EARLY * PIECE)
    pltpu.make_async_copy(c_part.at[early], c_ref.at[early], sem).start()
    for i in range(EARLY, SUBS):
        rows = pl.ds(i * PIECE, PIECE)
        done[rows] = c_part[rows] + jnp.dot(a_last[rows], b_last[...], preferred_element_type=jnp.float32)
        pltpu.make_async_copy(done.at[rows], c_ref.at[rows], sem).start()
    pltpu.make_async_copy(c_part, c_ref, sem).wait()


def solution(mesh):
    def local_product(a_blk, b_blk):
        rows, half = a_blk.shape
        piece = half // 2
        vmem = pl.BlockSpec(memory_space=pltpu.VMEM)
        hbm = pl.BlockSpec(memory_space=pltpu.HBM)
        parts = pl.pallas_call(
            _exchange,
            out_shape=[
                jax.ShapeDtypeStruct((rows, piece), jnp.float32),
                jax.ShapeDtypeStruct((rows, 4 * CHUNK), jnp.bfloat16),
                jax.ShapeDtypeStruct((4 * CHUNK, piece), jnp.bfloat16),
            ],
            in_specs=[hbm, hbm],
            out_specs=[vmem] * 3,
            scratch_shapes=[
                pltpu.VMEM((LAST, rows, 4 * CHUNK), jnp.bfloat16),
                pltpu.VMEM((LAST, 4 * CHUNK, piece), jnp.bfloat16),
                pltpu.SemaphoreType.DMA((RING + 1,)),
                pltpu.SemaphoreType.DMA((STEP_RING + 1,)),
                pltpu.SemaphoreType.DMA((B_RING,)),
                pltpu.SemaphoreType.DMA((STEP_RING + 1,)),
                pltpu.SemaphoreType.DMA((2,)),
                pltpu.SemaphoreType.DMA((4,)),
                pltpu.SemaphoreType.REGULAR((3,)),
            ],
            compiler_params=pltpu.CompilerParams(collective_id=0, has_side_effects=True, vmem_limit_bytes=LIMIT),
        )(a_blk, b_blk)
        return pl.pallas_call(
            _finish,
            out_shape=jax.ShapeDtypeStruct((rows, piece), jnp.float32),
            in_specs=[vmem] * 3,
            out_specs=hbm,
            scratch_shapes=[pltpu.VMEM((rows, piece), jnp.float32), pltpu.SemaphoreType.DMA],
            compiler_params=pltpu.CompilerParams(vmem_limit_bytes=LIMIT_FINISH),
        )(*parts)

    return jax.shard_map(
        local_product,
        mesh=mesh,
        in_specs=(P("row", "col"), P("row", "col")),
        out_specs=P("row", ("col", "dep")),
        check_vma=False,
    )
```

time: 81.6 us -> 80.2 us (0.983)
  Pallas kernels: 81.5 us -> 80.1 us
    pallas_call x1, Pallas kernels: 78.3 us -> 77.3 us  [local_product(): pl.pallas_call(_exchange, out_shape=[jax.ShapeDtypeStruct((rows, piece),...]
where the time goes in v3:
time: 80.2 us; the launch traced here: 80.1 us
  Pallas kernels  80.1 us (100%)
    pallas_call x1, Pallas kernels, local_product(): pl.pallas_call(_exchange, out_shape=[jax.ShapeDtypeStruct((rows, piece),...  77.3 us
    pallas_call x1, Pallas kernels, local_product(): pl.pallas_call(_finish, out_shape=jax.ShapeDtypeStruct((rows, piece), jnp...  2.76 us

profile of v3, /device:TPU:0, one launch (start us, length us, event | category | flops | bytes accessed | tf_op | source)
XLA Modules:
  0.0 80.1 jit_solution(7852754703912849475)
XLA Ops:
  0.0 77.3 %shard_map.28 = (f32[1280,1280]{1,0:T(8,128)S(1)}, bf16[1280,512]{1,0:T(8,128)(2,1)S(1)}, bf16[512,1280]{1,0:T(8,128)(2,1)S(1)}) custom-call(bf16[1280,2560]{1,0:T(8,128)(2,1)} %a_ref.1, bf16[1280,2560]{1,0:T(8,128)(2,1)} %b_ref.1), custom_call_target="tpu_custom_call" | custom-call | tf_op jit(solution)/shard_map/pallas_call | solution.py:240
  77.4 2.8 %shard_map.29 = f32[1280,1280]{1,0:T(8,128)} custom-call(f32[1280,1280]{1,0:T(8,128)S(1)} %get-tuple-element.8.c_part, bf16[1280,512]{1,0:T(8,128)(2,1)S(1)} %get-tuple-element.9.a_last, bf16[512,1280]{1,0:T(8,128)(2,1)S(1)} %get-tuple-element.10.b_last), custom_call_target="tpu_custom_call" | custom-call | tf_op jit(solution)/shard_map/pallas_call | solution.py:262

commit v4 on v3

--- a/solution.py
+++ b/solution.py
@@ -13,8 +13,8 @@
 COLS = 256
 TOTAL = STEPS * SUBS
 LAST = STEPS - 1
-EXTRA = 384
-EARLY = 3
+EXTRA = 416
+EARLY = 2
 AHEAD = 7
 WIDE = 5
 B_AHEAD = 2
@@ -116,7 +116,11 @@
             src = b_ref.at[pl.ds(t * CHUNK, CHUNK), aligned(z * quarter, quarter)]
             dst = b_step(t).at[lanes(r)]
             pltpu.make_async_copy(src, dst, local.at[1]).start()
-            remote(src, dst, local.at[2], local.at[3], to_d).start()
+
+    def start_peer():
+        for t in range(STEPS):
+            src = b_ref.at[pl.ds(t * CHUNK, CHUNK), aligned(z * quarter, quarter)]
+            remote(src, b_step(t).at[lanes(r)], local.at[2], local.at[3], to_d).start()
 
     def wait_local():
         take(a_ref, local.at[0])
@@ -127,8 +131,8 @@
         cols = pl.ds(p * COLS, COLS)
         c_ref[:, cols] += jnp.dot(abuf[t], bbuf[t, :, cols], preferred_element_type=jnp.float32)
 
-    x = r // 2
-    axes = ((x, to_x), (y, to_y), (z, to_z))
+    x, core = r // 2, lax.rem(r, 2)
+    axes = ((x, to_x), (y, to_y), (z, to_z), (1 - core, to_d))
     barrier = pltpu.get_barrier_semaphore()
     for at, to in axes:
 
@@ -136,8 +140,8 @@
         def _(to=to):
             pl.semaphore_signal(barrier, inc=1, device_id=to, device_id_type=MESH)
 
-    pl.semaphore_signal(barrier, inc=1, device_id=to_d, device_id_type=MESH)
-    pl.semaphore_wait(barrier, 1 + x + y + z)
+    ahead = x + y + z + 1 - core
+    pl.when(ahead > 0)(lambda: pl.semaphore_wait(barrier, ahead))
     for i, (at, to) in enumerate(axes):
 
         @pl.when(at == 1)
@@ -151,6 +155,8 @@
     pl.when(y == 1)(lambda: begin(1))
     pl.when(x == 1)(lambda: begin(0))
     start_local()
+    pl.when(core == 1)(lambda: pl.semaphore_wait(ready.at[3], 1))
+    start_peer()
     for i in (1, 0):
 
         @pl.when(axes[i][0] == 0)
@@ -255,7 +261,7 @@
                 pltpu.SemaphoreType.DMA((STEP_RING + 1,)),
                 pltpu.SemaphoreType.DMA((2,)),
                 pltpu.SemaphoreType.DMA((4,)),
-                pltpu.SemaphoreType.REGULAR((3,)),
+                pltpu.SemaphoreType.REGULAR((4,)),
             ],
             compiler_params=pltpu.CompilerParams(collective_id=0, has_side_effects=True, vmem_limit_bytes=LIMIT),
         )(a_blk, b_blk)

time: 80.2 us -> 80.1 us (level)
  no operation moved by 1% of the time
where the time goes in v4:
time: 80.1 us; the launch traced here: 79.9 us
  Pallas kernels  79.9 us (100%)
    pallas_call x1, Pallas kernels, local_product(): pl.pallas_call(_exchange, out_shape=[jax.ShapeDtypeStruct((rows, piece),...  77.2 us
    pallas_call x1, Pallas kernels, local_product(): pl.pallas_call(_finish, out_shape=jax.ShapeDtypeStruct((rows, piece), jnp...  2.76 us

profile of v4, /device:TPU:0, one launch (start us, length us, event | category | flops | bytes accessed | tf_op | source)
XLA Modules:
  0.0 79.9 jit_solution(413115401836050531)
XLA Ops:
  0.0 77.2 %shard_map.28 = (f32[1280,1280]{1,0:T(8,128)S(1)}, bf16[1280,512]{1,0:T(8,128)(2,1)S(1)}, bf16[512,1280]{1,0:T(8,128)(2,1)S(1)}) custom-call(bf16[1280,2560]{1,0:T(8,128)(2,1)} %a_ref.1, bf16[1280,2560]{1,0:T(8,128)(2,1)} %b_ref.1), custom_call_target="tpu_custom_call" | custom-call | tf_op jit(solution)/shard_map/pallas_call | solution.py:246
  77.2 2.8 %shard_map.29 = f32[1280,1280]{1,0:T(8,128)} custom-call(f32[1280,1280]{1,0:T(8,128)S(1)} %get-tuple-element.8.c_part, bf16[1280,512]{1,0:T(8,128)(2,1)S(1)} %get-tuple-element.9.a_last, bf16[512,1280]{1,0:T(8,128)(2,1)S(1)} %get-tuple-element.10.b_last), custom_call_target="tpu_custom_call" | custom-call | tf_op jit(solution)/shard_map/pallas_call | solution.py:268

commit v5 on v4

--- a/solution.py
+++ b/solution.py
@@ -13,11 +13,13 @@
 COLS = 256
 TOTAL = STEPS * SUBS
 LAST = STEPS - 1
-EXTRA = 416
+EXTRA = 448
 EARLY = 2
 AHEAD = 7
 WIDE = 5
 B_AHEAD = 2
+FIRST_HALF = (91, 93, 95, 97, 97)
+SECOND_HALF = (97, 98, 98, 99, 99)
 LAG = 6
 RING = 2 * AHEAD
 B_RING = 2 * B_AHEAD
@@ -133,6 +135,10 @@
 
     x, core = r // 2, lax.rem(r, 2)
     axes = ((x, to_x), (y, to_y), (z, to_z), (1 - core, to_d))
+    def half_product(t, p, side):
+        cols, half = pl.ds(p * COLS, COLS), aligned(side * 2 * CHUNK, 2 * CHUNK)
+        c_ref[:, cols] += jnp.dot(abuf[t, :, half], bbuf[t, half, cols], preferred_element_type=jnp.float32)
+
     barrier = pltpu.get_barrier_semaphore()
     for at, to in axes:
 
@@ -198,22 +204,27 @@
 
     lax.fori_loop(0, TAIL // SUBS, body, 0)
 
-    work = [(t, p) for t in (STEPS - 4, STEPS - 3, STEPS - 2) for p in range(SUBS // 2)]
-    begun = TAIL - (STEPS - 3) * SUBS - LAG
-    work = work[(begun + 1) // 2 :]
+    prior = LAST - 1
+    work = {}
+    for t in (prior - 2, prior - 1):
+        for p in range(SUBS // 2):
+            work.setdefault((t + 1) * SUBS + LAG + 2 * p, []).append((t, p, None))
+    for p in range(SUBS // 2):
+        work.setdefault(FIRST_HALF[p], []).append((prior, p, 0))
+        work.setdefault(SECOND_HALF[p], []).append((prior, p, 1))
     for n in range(TAIL, TOTAL):
         forward(n // SUBS, n % SUBS)
-        t, p = work[0] if work else (LAST, 0)
-        first = (t + 1) * SUBS + LAG
-        if t < LAST and n >= first + (2 * p if t < LAST - 1 else p):
-            if p == 0:
-                settle(t)
-            product(t, p)
-            work.pop(0)
-    for t, p in work:
-        if p == 0:
-            settle(t)
-        product(t, p)
+        for t, p, half in work.get(n, ()):
+            if half is None:
+                if p == 0:
+                    settle(t)
+                product(t, p)
+                continue
+            if p == 0 and half == 0:
+                take(bbuf.at[t, lanes(peer_across)], step_sem(dr, t))
+            if p == 0 and half == 1:
+                take(abuf.at[t, :, lanes(2 * (1 - y) + 1 - z)], step_sem(zr, t))
+            half_product(t, p, (y, 1 - y)[half])
     mine = lanes(2 * (1 - y) + 1 - z)
     early = EARLY * PIECE
     take(b_last.at[lanes(peer_across)], step_sem(dr, LAST))

time: 80.1 us -> 79.9 us (level)
  no operation moved by 1% of the time
where the time goes in v5:
time: 79.9 us; the launch traced here: 79.8 us
  Pallas kernels  79.8 us (100%)
    pallas_call x1, Pallas kernels, local_product(): pl.pallas_call(_exchange, out_shape=[jax.ShapeDtypeStruct((rows, piece),...  77 us
    pallas_call x1, Pallas kernels, local_product(): pl.pallas_call(_finish, out_shape=jax.ShapeDtypeStruct((rows, piece), jnp...  2.76 us

profile of v5, /device:TPU:0, one launch (start us, length us, event | category | flops | bytes accessed | tf_op | source)
XLA Modules:
  0.0 79.8 jit_solution(14676565019545722994)
XLA Ops:
  0.0 77.0 %shard_map.28 = (f32[1280,1280]{1,0:T(8,128)S(1)}, bf16[1280,512]{1,0:T(8,128)(2,1)S(1)}, bf16[512,1280]{1,0:T(8,128)(2,1)S(1)}) custom-call(bf16[1280,2560]{1,0:T(8,128)(2,1)} %a_ref.1, bf16[1280,2560]{1,0:T(8,128)(2,1)} %b_ref.1), custom_call_target="tpu_custom_call" | custom-call | tf_op jit(solution)/shard_map/pallas_call | solution.py:257
  77.0 2.8 %shard_map.29 = f32[1280,1280]{1,0:T(8,128)} custom-call(f32[1280,1280]{1,0:T(8,128)S(1)} %get-tuple-element.8.c_part, bf16[1280,512]{1,0:T(8,128)(2,1)S(1)} %get-tuple-element.9.a_last, bf16[512,1280]{1,0:T(8,128)(2,1)S(1)} %get-tuple-element.10.b_last), custom_call_target="tpu_custom_call" | custom-call | tf_op jit(solution)/shard_map/pallas_call | solution.py:279

commit v6 on v5

--- a/solution.py
+++ b/solution.py
@@ -117,17 +117,16 @@
                 pltpu.make_async_copy(src, a_step(t).at[:, lanes(2 * y + part)], local.at[0]).start()
             src = b_ref.at[pl.ds(t * CHUNK, CHUNK), aligned(z * quarter, quarter)]
             dst = b_step(t).at[lanes(r)]
-            pltpu.make_async_copy(src, dst, local.at[1]).start()
+            pltpu.make_async_copy(src, dst, local.at[0]).start()
 
     def start_peer():
         for t in range(STEPS):
             src = b_ref.at[pl.ds(t * CHUNK, CHUNK), aligned(z * quarter, quarter)]
-            remote(src, b_step(t).at[lanes(r)], local.at[2], local.at[3], to_d).start()
+            remote(src, b_step(t).at[lanes(r)], sent.at[1], local.at[1], to_d).start()
 
     def wait_local():
-        take(a_ref, local.at[0])
-        for i in (1, 2, 3):
-            take(b_ref.at[:, pl.ds(0, quarter)], local.at[i])
+        take(abuf.at[pl.ds(0, 8), pl.ds(0, 1200)], local.at[0])
+        take(b_ref.at[:, pl.ds(0, quarter)], local.at[1])
 
     def product(t, p):
         cols = pl.ds(p * COLS, COLS)
@@ -235,7 +234,7 @@
     take(a_last.at[pl.ds(early, SUBS * PIECE - EXTRA - early), mine], step_sem(zr, LAST))
     take(a_last.at[pl.ds(SUBS * PIECE - EXTRA, EXTRA), mine], yr.at[RING])
     take(a_ref, sent.at[0])
-    take(b_ref, sent.at[1])
+    take(abuf.at[pl.ds(0, 8), pl.ds(0, 1200)], sent.at[1])
 
 
 def _finish(c_part, a_last, b_last, c_ref, done, sem):
@@ -271,7 +270,7 @@
                 pltpu.SemaphoreType.DMA((B_RING,)),
                 pltpu.SemaphoreType.DMA((STEP_RING + 1,)),
                 pltpu.SemaphoreType.DMA((2,)),
-                pltpu.SemaphoreType.DMA((4,)),
+                pltpu.SemaphoreType.DMA((2,)),
                 pltpu.SemaphoreType.REGULAR((4,)),
             ],
             compiler_params=pltpu.CompilerParams(collective_id=0, has_side_effects=True, vmem_limit_bytes=LIMIT),

time: 79.9 us -> 79.9 us (level)
  no operation moved by 1% of the time
where the time goes in v6:
time: 79.9 us; the launch traced here: 79.8 us
  Pallas kernels  79.7 us (100%)
    pallas_call x1, Pallas kernels, local_product(): pl.pallas_call(_exchange, out_shape=[jax.ShapeDtypeStruct((rows, piece),...  77 us
    pallas_call x1, Pallas kernels, local_product(): pl.pallas_call(_finish, out_shape=jax.ShapeDtypeStruct((rows, piece), jnp...  2.76 us

profile of v6, /device:TPU:0, one launch (start us, length us, event | category | flops | bytes accessed | tf_op | source)
XLA Modules:
  0.0 79.8 jit_solution(2299290340592614521)
XLA Ops:
  0.0 77.0 %shard_map.28 = (f32[1280,1280]{1,0:T(8,128)S(1)}, bf16[1280,512]{1,0:T(8,128)(2,1)S(1)}, bf16[512,1280]{1,0:T(8,128)(2,1)S(1)}) custom-call(bf16[1280,2560]{1,0:T(8,128)(2,1)} %a_ref.1, bf16[1280,2560]{1,0:T(8,128)(2,1)} %b_ref.1), custom_call_target="tpu_custom_call" | custom-call | tf_op jit(solution)/shard_map/pallas_call | solution.py:256
  77.0 2.8 %shard_map.29 = f32[1280,1280]{1,0:T(8,128)} custom-call(f32[1280,1280]{1,0:T(8,128)S(1)} %get-tuple-element.8.c_part, bf16[1280,512]{1,0:T(8,128)(2,1)S(1)} %get-tuple-element.9.a_last, bf16[512,1280]{1,0:T(8,128)(2,1)S(1)} %get-tuple-element.10.b_last), custom_call_target="tpu_custom_call" | custom-call | tf_op jit(solution)/shard_map/pallas_call | solution.py:278

commit v7 on v6

--- a/solution.py
+++ b/solution.py
@@ -75,7 +75,7 @@
         if isinstance(n, int) and n == TOTAL:
             rows = pl.ds(SUBS * PIECE - EXTRA, EXTRA)
             src = a_ref.at[rows, aligned((1 - z) * quarter + LAST * CHUNK, CHUNK)]
-            remote(src, a_last.at[rows, lanes(2 * y + 1 - z)], sent.at[0], yr.at[RING], to_y).start()
+            remote(src, a_last.at[rows, lanes(2 * y + 1 - z)], sent.at[0], step_sem(zr, LAST), to_y).start()
             return
         src = a_ref.at[aligned((n % SUBS) * PIECE, PIECE), aligned(z * quarter + n // SUBS * CHUNK, CHUNK)]
         remote(src, a_slot(n, 2 * y + z), sent.at[0], yr.at[lax.rem(n, RING)], to_y).start()
@@ -104,7 +104,8 @@
 
     def d_start(n):
         slot = b_slot(n, across)
-        remote(slot, slot, sent.at[1], step_sem(dr, n // B_SUBS), to_d).start()
+        t = n // B_SUBS
+        remote(slot, slot, sent.at[1], zr.at[STEP_RING] if is_last(t) else step_sem(dr, t), to_d).start()
 
     def settle(t):
         take(abuf.at[t, :, lanes(2 * (1 - y) + 1 - z)], step_sem(zr, t))
@@ -226,13 +227,12 @@
             half_product(t, p, (y, 1 - y)[half])
     mine = lanes(2 * (1 - y) + 1 - z)
     early = EARLY * PIECE
-    take(b_last.at[lanes(peer_across)], step_sem(dr, LAST))
-    take(a_last.at[pl.ds(0, early), mine], zr.at[STEP_RING])
+    assert early * CHUNK + CHUNK * quarter == (early // 4 + quarter // 4) * 4 * CHUNK
+    take(a_last.at[pl.ds(0, early // 4 + quarter // 4)], zr.at[STEP_RING])
     for i in range(EARLY):
         rows = pl.ds(i * PIECE, PIECE)
         c_ref[rows] += jnp.dot(a_last[rows], b_last[...], preferred_element_type=jnp.float32)
-    take(a_last.at[pl.ds(early, SUBS * PIECE - EXTRA - early), mine], step_sem(zr, LAST))
-    take(a_last.at[pl.ds(SUBS * PIECE - EXTRA, EXTRA), mine], yr.at[RING])
+    take(a_last.at[pl.ds(early, SUBS * PIECE - early), mine], step_sem(zr, LAST))
     take(a_ref, sent.at[0])
     take(abuf.at[pl.ds(0, 8), pl.ds(0, 1200)], sent.at[1])
 
@@ -265,7 +265,7 @@
             scratch_shapes=[
                 pltpu.VMEM((LAST, rows, 4 * CHUNK), jnp.bfloat16),
                 pltpu.VMEM((LAST, 4 * CHUNK, piece), jnp.bfloat16),
-                pltpu.SemaphoreType.DMA((RING + 1,)),
+                pltpu.SemaphoreType.DMA((RING,)),
                 pltpu.SemaphoreType.DMA((STEP_RING + 1,)),
                 pltpu.SemaphoreType.DMA((B_RING,)),
                 pltpu.SemaphoreType.DMA((STEP_RING + 1,)),

time: 79.9 us -> 79.9 us (level)
  no operation moved by 1% of the time
where the time goes in v7:
time: 79.9 us; the launch traced here: 79.7 us
  Pallas kernels  79.7 us (100%)
    pallas_call x1, Pallas kernels, local_product(): pl.pallas_call(_exchange, out_shape=[jax.ShapeDtypeStruct((rows, piece),...  77 us
    pallas_call x1, Pallas kernels, local_product(): pl.pallas_call(_finish, out_shape=jax.ShapeDtypeStruct((rows, piece), jnp...  2.76 us

profile of v7, /device:TPU:0, one launch (start us, length us, event | category | flops | bytes accessed | tf_op | source)
XLA Modules:
  0.0 79.7 jit_solution(15301522166078081236)
XLA Ops:
  0.0 77.0 %shard_map.28 = (f32[1280,1280]{1,0:T(8,128)S(1)}, bf16[1280,512]{1,0:T(8,128)(2,1)S(1)}, bf16[512,1280]{1,0:T(8,128)(2,1)S(1)}) custom-call(bf16[1280,2560]{1,0:T(8,128)(2,1)} %a_ref.1, bf16[1280,2560]{1,0:T(8,128)(2,1)} %b_ref.1), custom_call_target="tpu_custom_call" | custom-call | tf_op jit(solution)/shard_map/pallas_call | solution.py:256
  77.0 2.8 %shard_map.29 = f32[1280,1280]{1,0:T(8,128)} custom-call(f32[1280,1280]{1,0:T(8,128)S(1)} %get-tuple-element.8.c_part, bf16[1280,512]{1,0:T(8,128)(2,1)S(1)} %get-tuple-element.9.a_last, bf16[512,1280]{1,0:T(8,128)(2,1)S(1)} %get-tuple-element.10.b_last), custom_call_target="tpu_custom_call" | custom-call | tf_op jit(solution)/shard_map/pallas_call | solution.py:278

commit v8 on v7

--- a/solution.py
+++ b/solution.py
@@ -13,7 +13,7 @@
 COLS = 256
 TOTAL = STEPS * SUBS
 LAST = STEPS - 1
-EXTRA = 448
+EXTRA = 464
 EARLY = 2
 AHEAD = 7
 WIDE = 5

time: 79.9 us -> 79.9 us (level)
  no operation moved by 1% of the time
where the time goes in v8:
time: 79.9 us; the launch traced here: 79.8 us
  Pallas kernels  79.8 us (100%)
    pallas_call x1, Pallas kernels, local_product(): pl.pallas_call(_exchange, out_shape=[jax.ShapeDtypeStruct((rows, piece),...  77 us
    pallas_call x1, Pallas kernels, local_product(): pl.pallas_call(_finish, out_shape=jax.ShapeDtypeStruct((rows, piece), jnp...  2.76 us

profile of v8, /device:TPU:0, one launch (start us, length us, event | category | flops | bytes accessed | tf_op | source)
XLA Modules:
  0.0 79.8 jit_solution(6354958523990753234)
XLA Ops:
  0.0 77.0 %shard_map.28 = (f32[1280,1280]{1,0:T(8,128)S(1)}, bf16[1280,512]{1,0:T(8,128)(2,1)S(1)}, bf16[512,1280]{1,0:T(8,128)(2,1)S(1)}) custom-call(bf16[1280,2560]{1,0:T(8,128)(2,1)} %a_ref.1, bf16[1280,2560]{1,0:T(8,128)(2,1)} %b_ref.1), custom_call_target="tpu_custom_call" | custom-call | tf_op jit(solution)/shard_map/pallas_call | solution.py:256
  77.0 2.8 %shard_map.29 = f32[1280,1280]{1,0:T(8,128)} custom-call(f32[1280,1280]{1,0:T(8,128)S(1)} %get-tuple-element.8.c_part, bf16[1280,512]{1,0:T(8,128)(2,1)S(1)} %get-tuple-element.9.a_last, bf16[512,1280]{1,0:T(8,128)(2,1)S(1)} %get-tuple-element.10.b_last), custom_call_target="tpu_custom_call" | custom-call | tf_op jit(solution)/shard_map/pallas_call | solution.py:278
